TPU v7x, 512 devices: a whole 4x4x16 slice. The times are simulated.
512 devices in a mesh: blk: 16 (over x_lo, y, core), group: 32 (over x_hi, z).
Axes of the slice: x: 4 (x_hi: 2, x_lo: 2; x = x_hi * 2 + x_lo), y: 4, z: 16, core: 2. Of those that a mesh axis runs over, the one named last changes fastest.
Arguments:
- queries: bfloat16 [512, 16, 128], P(('blk', 'group')), may hold values from -2.5 to 2.5
- query_mask: int32 [512, 16], P(('blk', 'group')), may hold values from 0 to 1, as said below
- positive: int32 [512], P(('blk', 'group')), may hold values from 0 to 1023
- page_vectors: bfloat16 [1024, 128, 128], P(('blk', 'group')), may hold values from -2 to 2
- page_mask: int32 [1024, 128], P(('blk', 'group')), may hold values from 0 to 1, as said below
Outputs:
- grad_queries: float32 [512, 16, 128], P(('blk', 'group'))
- grad_pages: float32 [1024, 128, 128], P(('blk', 'group'))
- mean_loss: float32 [], replicated
Inputs may be any that keep to these rules, and one draw needn't show every extreme that they name: `query_mask`: each row holds ones on its first 8 to 16 token slots and zeros after them. `page_mask`: each row holds ones on its first 32 to 128 patch slots and zeros after them.
All inputs are finite; a program needn't handle non-finite values.
Results may differ from a plain program's by a relative error of at most 0.0028.
Values may be sent and summed in bfloat16 or wider, within the bound.
A program may use at most 64 MiB of HBM per device.

v0:
```python
import functools
import math
import jax
import jax.numpy as jnp
from jax import lax
from jax.sharding import Mesh
from jax.sharding import PartitionSpec as P

BLK = ("blk_0", "blk_1", "blk_2")
GROUP = ("group_0", "group_1")
BLK_GROUP = ("blk_0", "blk_1", "blk_2", "group_0", "group_1")
relaxation_scale_factor = 0.5
guarded_floor_entry = -1e30


def side_by_side(arrays, axis, dim, along):
    columns = [a.reshape(*a.shape[:along], -1) for a in arrays]
    both = jnp.concatenate(columns, axis=along)
    result, at, gathered = (lax.all_gather(both, axis, axis=dim, tiled=True), 0, [])
    for a, column in zip(arrays, columns):
        section = result[..., at : at + column.shape[along]]
        gathered.append(section.reshape(*section.shape[:along], *a.shape[along:]))
        at += column.shape[along]
    return tuple(gathered)


def over_axes(x, axes):
    return functools.reduce(lax.pmax, axes, x)


def one_axis_at_a_time(x, axes):
    for axis in axes:
        x = lax.psum(x, axis)
    return x


def from_behind(value, axis, steps):
    count = lax.axis_size(axis)
    pairs = [(source, (source + steps) % count) for source in range(count)]
    return lax.ppermute(value, axis, pairs)


def cut_along(x, dim, size):
    before, after = (x.shape[:dim], x.shape[dim + 1 :])
    return jnp.moveaxis(x.reshape(*before, size, -1, *after), dim, 0)


def sum_at_owner(x, axis, dim):
    size = lax.axis_size(axis)
    pieces = lax.all_to_all(cut_along(x, dim, size), axis, 0, 0, tiled=True)
    return jnp.sum(pieces, axis=0)


def masked_logits(row_block, lone_document, live_image_embeddings):
    similarity_matrix = lax.dot_general(
        row_block, lone_document, (((1,), (1,)), ((), ())), preferred_element_type=jnp.float32
    )
    return jnp.where(
        live_image_embeddings[None, :] > 0,
        similarity_matrix / relaxation_scale_factor,
        guarded_floor_entry,
    )


def on_device(queries, query_mask, positive, page_vectors, page_mask):
    tokens = queries.shape[1]
    features = queries.shape[2]
    local_pages = page_vectors.shape[0]
    blocks = lax.axis_size(BLK)
    members = lax.axis_size(GROUP)
    bundle_size = queries.shape[0] * members
    total_queries = bundle_size * blocks
    natural_logarithm_lengths = jnp.log(jnp.sum(page_mask.astype(jnp.float32), axis=1))
    bundle_vectors, bundle_masks, bundle_targets = (
        lax.all_gather(queries, GROUP, axis=0, tiled=True),
        *side_by_side((query_mask, positive), GROUP, 0, 1),
    )

    def forward_piece(folded, shard_in, root_row):
        scores, lse_rows, live_all, owners, kept = folded
        vectors, token_masks, targets = shard_in
        amount = vectors.shape[0]
        stride = math.gcd(amount, max(1, 512 // tokens))

        def run_block(number, current):
            scores, lse_rows = current
            offset = number * stride
            slab_rows = lax.dynamic_slice_in_dim(vectors, offset, stride, 0).reshape(
                stride * tokens, features
            )
            alive = lax.dynamic_slice_in_dim(token_masks, offset, stride, 0).astype(jnp.float32)
            found_sums = []
            for index_page in range(local_pages):
                masked = masked_logits(slab_rows, page_vectors[index_page], page_mask[index_page])
                highest = jnp.max(masked, axis=1, keepdims=True)
                found_sums.append(
                    highest[:, 0] + jnp.log(jnp.sum(jnp.exp(masked - highest), axis=1))
                )
            logsumexp_results = jnp.stack(found_sums, axis=1).reshape(stride, tokens, local_pages)
            softened_supremum = relaxation_scale_factor * (
                logsumexp_results - natural_logarithm_lengths
            )
            page_score = jnp.sum(alive[:, :, None] * softened_supremum, axis=1)
            scores = lax.dynamic_update_slice_in_dim(scores, page_score, offset, 0)
            lse_rows = lax.dynamic_update_slice_in_dim(lse_rows, logsumexp_results, offset, 0)
            return (scores, lse_rows)

        scores, lse_rows = lax.fori_loop(0, amount // stride, run_block, (scores, lse_rows))
        live_all = lax.dynamic_update_slice_in_dim(live_all, token_masks, root_row, 0)
        owners = lax.dynamic_update_slice_in_dim(owners, targets, root_row, 0)
        kept = vectors
        return (scores, lse_rows, live_all, owners, kept)

    starting = (
        jnp.zeros((total_queries, local_pages), jnp.float32),
        jnp.zeros((total_queries, tokens, local_pages), jnp.float32),
        jnp.zeros((total_queries, tokens), jnp.int32),
        jnp.zeros((total_queries,), jnp.int32),
        jnp.zeros((total_queries, tokens, features), jnp.bfloat16),
    )
    scores, lse_rows, live_all, owners, kept = forward_piece(
        starting,
        (
            lax.all_gather(bundle_vectors, BLK, axis=0, tiled=True),
            lax.all_gather(bundle_masks, BLK, axis=0, tiled=True),
            lax.all_gather(bundle_targets, BLK, axis=0, tiled=True),
        ),
        jnp.int32(0),
    )
    position = lax.axis_index(BLK_GROUP)
    page_ids = position * local_pages + jnp.arange(local_pages, dtype=jnp.int32)
    chosen = owners[:, None] == page_ids[None, :]
    picked_local = jnp.sum(jnp.where(chosen, scores, 0.0))
    local_top = jnp.max(scores, axis=1)
    highest = over_axes(local_top, BLK_GROUP)
    local_total = jnp.sum(jnp.exp(scores - highest[:, None]), axis=1)
    totals, picked = (
        one_axis_at_a_time(local_total, BLK_GROUP),
        one_axis_at_a_time(picked_local, BLK_GROUP),
    )
    page_lse = highest + jnp.log(totals)
    mean_loss = (jnp.sum(page_lse) - picked) / total_queries
    coefficient = jnp.exp(scores - page_lse[:, None]) - chosen.astype(jnp.float32)
    factor_scale = coefficient[:, None, :] * live_all.astype(jnp.float32)[:, :, None]

    def slice_rows(root_row, amount):
        sums = lax.dynamic_slice_in_dim(lse_rows, root_row, amount, 0).reshape(
            amount * tokens, local_pages
        )
        scales = lax.dynamic_slice_in_dim(factor_scale, root_row, amount, 0).reshape(
            amount * tokens, local_pages
        )
        return (sums, scales)

    def gradient_terms(row_block, logsumexp_results, scales, page_grads):
        partial_value = jnp.zeros(row_block.shape, jnp.float32)
        for number in range(local_pages):
            masked = masked_logits(row_block, page_vectors[number], page_mask[number])
            weights = jnp.exp(masked - logsumexp_results[:, number : number + 1])
            factor = (scales[:, number : number + 1] * weights).astype(jnp.bfloat16)
            partial_value = partial_value + jnp.dot(
                factor, page_vectors[number], preferred_element_type=jnp.float32
            )
            update = lax.dot_general(
                factor, row_block, (((0,), (0,)), ((), ())), preferred_element_type=jnp.float32
            )
            page_grads = page_grads.at[number].add(update)
        return (partial_value, page_grads)

    home = lax.axis_index(BLK)
    page_grads = jnp.zeros(page_vectors.shape, jnp.float32)

    def visit_one(moving, collected, page_grads, lap_index):
        root_row = (home - lap_index) % blocks * bundle_size
        sums, scales = slice_rows(root_row, bundle_size)
        partial_value, page_grads = gradient_terms(
            moving.reshape(bundle_size * tokens, features), sums, scales, page_grads
        )
        return (collected + partial_value.reshape(bundle_size, tokens, features), page_grads)

    def pass_one(collected):
        return from_behind(collected, BLK, 1)

    def turn_one(lap_index, current):
        moving, collected, page_grads = current
        collected, page_grads = visit_one(moving, collected, page_grads, lap_index)
        moving = from_behind(moving, BLK, 1)
        return (moving, pass_one(collected), page_grads)

    empty_whole = jnp.zeros((bundle_size, tokens, features), jnp.float32)
    moving, collected, page_grads = lax.fori_loop(
        0, blocks - 1, turn_one, (bundle_vectors, empty_whole, page_grads)
    )
    collected, page_grads = visit_one(moving, collected, page_grads, blocks - 1)
    collected = pass_one(collected)
    grad_queries = sum_at_owner(collected, GROUP, 0)
    return (grad_queries, page_grads, mean_loss)


def solution(mesh):
    split = Mesh(
        mesh.devices.reshape(2, 4, 2, 2, 16), ("blk_0", "blk_1", "blk_2", "group_0", "group_1")
    )
    return jax.shard_map(
        on_device,
        mesh=split,
        in_specs=(
            P(BLK_GROUP, None, None),
            P(BLK_GROUP, None),
            P(BLK_GROUP),
            P(BLK_GROUP, None, None),
            P(BLK_GROUP, None),
        ),
        out_specs=(P(BLK_GROUP, None, None), P(BLK_GROUP, None, None), P()),
        check_vma=False,
    )
```

profile of v0, /device:TPU:2, one launch (start us, length us, event | category | flops | bytes accessed | tf_op | source)
XLA Modules:
  0.0 667.9 jit_solution(16827437556974625158)
XLA Ops:
  7.2 87.3 %all_gather.15 = bf16[32,16,128]{2,1,0:T(8,128)(2,1)} all-gather(bf16[1,16,128]{2,1,0:T(8,128)(2,1)} %param.17), channel_id=1, replica_groups=mesh['blk_0'=2,'blk_1'=4,'blk_2'=2,'group_0'=2,'group_1'=16] {'group_0',..., dimensions={0}, use_global_device_ids=true | all-gather | bytes 135168 | tf_op jit(solution)/shard_map/all_gather | solution.py:75
  95.9 70.5 %all-gather.1 = s32[32,1,17]{2,1,0:T(1,128)S(1)} all-gather(s32[1,1,17]{2,1,0:T(1,128)S(1)} %add_bitcast_fusion), channel_id=1, replica_groups=mesh['blk_0'=2,'blk_1'=4,'blk_2'=2,'group_0'=2,'group_1'=16] {'group_0',..., dimensions={0}, use_global_device_ids=true | all-gather | bytes 2244 | tf_op jit(solution)/shard_map/all_gather | solution.py:19
  166.4 20.1 %all-gather.2 = s32[16,32,16]{1,2,0:T(8,128)S(1)} all-gather(s32[1,32,16]{1,2,0:T(8,128)S(1)} %copy.11), channel_id=1, replica_groups=mesh['blk_0'=2,'blk_1'=4,'blk_2'=2,'group_0'=2,'group_1'=16] {'blk_0','b..., dimensions={0}, use_global_device_ids=true | all-gather | bytes 34816 | tf_op jit(solution)/shard_map/all_gather | solution.py:125
  190.0 8.0 %all-reduce = s32[512]{0:T(512)S(1)} all-reduce(s32[512]{0:T(512)S(1)} %dynamic-update-slice.26), channel_id=2, replica_groups=mesh['blk_0'=2,'blk_1'=4,'blk_2'=2,'group_0'=2,'group_1'=16] {'blk_0','b..., use_global_device_ids=true, to_apply=%add | all-reduce | flops 512 | bytes 4096
  198.9 72.4 %while.38 = (s32[]{:T(128)}, f32[512,2]{0,1:T(2,128)S(1)}, f32[512,16,2]{1,0,2:T(8,128)S(1)}, s32[2,128]{1,0:T(2,128)}, bf16[512,16,128]{2,1,0:T(8,128)(2,1)}, /...) while((s32[]{:T(128)}, f32[512,2]{0,1:T(2,128)S(1)}, ...), condition=%wide.region_7.8_spmd, body=%wide.region_1.7_spmd.sunk | while | flops 34213060 | bytes 1820339 | solution.py:108
  271.3 4.9 pmax.35
  276.2 11.6 %pmax.36 = f32[512]{0:T(512)S(1)} all-reduce(f32[512]{0:T(512)S(1)} %pmax.35), channel_id=1, replica_groups=mesh['blk_0'=2,'blk_1'=4,'blk_2'=2,'group_0'=2,'group_1'=16] {'blk_1'}, use_global_device_ids=true, to_apply=%region_10.11 | all-reduce | flops 512 | bytes 4096 | tf_op jit(solution)/shard_map/pmax | solution.py:28
  290.2 6.4 pmax.38
  296.7 29.0 %pmax.39 = f32[512]{0:T(512)S(1)} all-reduce(f32[512]{0:T(512)S(1)} %pmax.38), channel_id=1, replica_groups=mesh['blk_0'=2,'blk_1'=4,'blk_2'=2,'group_0'=2,'group_1'=16] {'group_1'}, use_global_device_ids=true, to_apply=%region_13.14 | all-reduce | flops 512 | bytes 4096 | tf_op jit(solution)/shard_map/pmax | solution.py:28
  326.4 5.5 all-reduce.5
  331.9 8.3 %all-reduce.2 = (f32[512]{0:T(512)S(1)}, f32[]{:T(128)}) all-reduce(f32[512]{0:T(512)S(1)} %get-tuple-element.502, f32[]{:T(128)} %get-tuple-element.503), channel_id=1, replica_groups=mesh['blk_0'=2,'blk_1'=4,'blk_2'=2,'group_0'=2,'group_1'=16] {'blk_1'}, use_global_device_ids=true, to_apply=%region_16.17 | all-reduce | flops 513 | bytes 4104 | tf_op jit(solution)/shard_map/psum | solution.py:33
  343.3 7.0 %all-reduce.3 = (f32[512]{0:T(512)S(1)}, f32[]{:T(128)}) all-reduce(f32[512]{0:T(512)S(1)} %get-tuple-element.500, f32[]{:T(128)} %get-tuple-element.501), channel_id=1, replica_groups=mesh['blk_0'=2,'blk_1'=4,'blk_2'=2,'group_0'=2,'group_1'=16] {'group_0'}, use_global_device_ids=true, to_apply=%region_18.19 | all-reduce | flops 513 | bytes 4104 | tf_op jit(solution)/shard_map/psum | solution.py:33
  350.4 27.6 %all-reduce.1 = (f32[512]{0:T(512)S(1)}, f32[]{:T(128)}) all-reduce(f32[512]{0:T(512)S(1)} %get-tuple-element.498, f32[]{:T(128)} %get-tuple-element.499), channel_id=1, replica_groups=mesh['blk_0'=2,'blk_1'=4,'blk_2'=2,'group_0'=2,'group_1'=16] {'group_1'}, use_global_device_ids=true, to_apply=%region_19.20 | all-reduce | flops 513 | bytes 4104 | tf_op jit(solution)/shard_map/psum | solution.py:33
  379.3 240.3 %while.39 = (s32[]{:T(128)}, bf16[32,16,128]{2,1,0:T(8,128)(2,1)S(1)}, f32[32,16,128]{2,1,0:T(8,128)S(1)}, f32[2,128,128]{2,1,0:T(8,128)S(1)}, s32[]{:T(128)}, /...) while((s32[]{:T(128)}, ...), condition=%wide.region_21.22_spmd, body=%wide.region_20.21_spmd.sunk | while | flops 101482768 | bytes 5433252 | solution.py:191
  389.9 5.3 collective-permute-done.1
  403.8 7.4 %collective-permute-done.1 = f32[32,16,128]{2,1,0:T(8,128)S(1)} collective-permute-done((f32[32,16,128]{2,1,0:T(8,128)S(1)}, f32[32,16,128]{2,1,0:T(8,128)S(1)}, u32[]{:S(2)}, u32[]{:S(2)}) %collective-permute-start.1) | collective-permute-done | bytes 262176 | tf_op jit(solution)/shard_map/while/body/eval_jaxpr/ppermute | solution.py:40
  419.8 7.4 %collective-permute-done.1 = f32[32,16,128]{2,1,0:T(8,128)S(1)} collective-permute-done((f32[32,16,128]{2,1,0:T(8,128)S(1)}, f32[32,16,128]{2,1,0:T(8,128)S(1)}, u32[]{:S(2)}, u32[]{:S(2)}) %collective-permute-start.1) | collective-permute-done | bytes 262176 | tf_op jit(solution)/shard_map/while/body/eval_jaxpr/ppermute | solution.py:40
  435.9 7.4 %collective-permute-done.1 = f32[32,16,128]{2,1,0:T(8,128)S(1)} collective-permute-done((f32[32,16,128]{2,1,0:T(8,128)S(1)}, f32[32,16,128]{2,1,0:T(8,128)S(1)}, u32[]{:S(2)}, u32[]{:S(2)}) %collective-permute-start.1) | collective-permute-done | bytes 262176 | tf_op jit(solution)/shard_map/while/body/eval_jaxpr/ppermute | solution.py:40
  451.9 7.4 %collective-permute-done.1 = f32[32,16,128]{2,1,0:T(8,128)S(1)} collective-permute-done((f32[32,16,128]{2,1,0:T(8,128)S(1)}, f32[32,16,128]{2,1,0:T(8,128)S(1)}, u32[]{:S(2)}, u32[]{:S(2)}) %collective-permute-start.1) | collective-permute-done | bytes 262176 | tf_op jit(solution)/shard_map/while/body/eval_jaxpr/ppermute | solution.py:40
  467.9 7.4 %collective-permute-done.1 = f32[32,16,128]{2,1,0:T(8,128)S(1)} collective-permute-done((f32[32,16,128]{2,1,0:T(8,128)S(1)}, f32[32,16,128]{2,1,0:T(8,128)S(1)}, u32[]{:S(2)}, u32[]{:S(2)}) %collective-permute-start.1) | collective-permute-done | bytes 262176 | tf_op jit(solution)/shard_map/while/body/eval_jaxpr/ppermute | solution.py:40
  483.9 7.4 %collective-permute-done.1 = f32[32,16,128]{2,1,0:T(8,128)S(1)} collective-permute-done((f32[32,16,128]{2,1,0:T(8,128)S(1)}, f32[32,16,128]{2,1,0:T(8,128)S(1)}, u32[]{:S(2)}, u32[]{:S(2)}) %collective-permute-start.1) | collective-permute-done | bytes 262176 | tf_op jit(solution)/shard_map/while/body/eval_jaxpr/ppermute | solution.py:40
  500.0 7.4 %collective-permute-done.1 = f32[32,16,128]{2,1,0:T(8,128)S(1)} collective-permute-done((f32[32,16,128]{2,1,0:T(8,128)S(1)}, f32[32,16,128]{2,1,0:T(8,128)S(1)}, u32[]{:S(2)}, u32[]{:S(2)}) %collective-permute-start.1) | collective-permute-done | bytes 262176 | tf_op jit(solution)/shard_map/while/body/eval_jaxpr/ppermute | solution.py:40
  516.0 7.4 %collective-permute-done.1 = f32[32,16,128]{2,1,0:T(8,128)S(1)} collective-permute-done((f32[32,16,128]{2,1,0:T(8,128)S(1)}, f32[32,16,128]{2,1,0:T(8,128)S(1)}, u32[]{:S(2)}, u32[]{:S(2)}) %collective-permute-start.1) | collective-permute-done | bytes 262176 | tf_op jit(solution)/shard_map/while/body/eval_jaxpr/ppermute | solution.py:40
  532.0 7.4 %collective-permute-done.1 = f32[32,16,128]{2,1,0:T(8,128)S(1)} collective-permute-done((f32[32,16,128]{2,1,0:T(8,128)S(1)}, f32[32,16,128]{2,1,0:T(8,128)S(1)}, u32[]{:S(2)}, u32[]{:S(2)}) %collective-permute-start.1) | collective-permute-done | bytes 262176 | tf_op jit(solution)/shard_map/while/body/eval_jaxpr/ppermute | solution.py:40
  548.0 7.4 %collective-permute-done.1 = f32[32,16,128]{2,1,0:T(8,128)S(1)} collective-permute-done((f32[32,16,128]{2,1,0:T(8,128)S(1)}, f32[32,16,128]{2,1,0:T(8,128)S(1)}, u32[]{:S(2)}, u32[]{:S(2)}) %collective-permute-start.1) | collective-permute-done | bytes 262176 | tf_op jit(solution)/shard_map/while/body/eval_jaxpr/ppermute | solution.py:40
  564.1 7.4 %collective-permute-done.1 = f32[32,16,128]{2,1,0:T(8,128)S(1)} collective-permute-done((f32[32,16,128]{2,1,0:T(8,128)S(1)}, f32[32,16,128]{2,1,0:T(8,128)S(1)}, u32[]{:S(2)}, u32[]{:S(2)}) %collective-permute-start.1) | collective-permute-done | bytes 262176 | tf_op jit(solution)/shard_map/while/body/eval_jaxpr/ppermute | solution.py:40
  580.1 7.4 %collective-permute-done.1 = f32[32,16,128]{2,1,0:T(8,128)S(1)} collective-permute-done((f32[32,16,128]{2,1,0:T(8,128)S(1)}, f32[32,16,128]{2,1,0:T(8,128)S(1)}, u32[]{:S(2)}, u32[]{:S(2)}) %collective-permute-start.1) | collective-permute-done | bytes 262176 | tf_op jit(solution)/shard_map/while/body/eval_jaxpr/ppermute | solution.py:40
  596.1 7.4 %collective-permute-done.1 = f32[32,16,128]{2,1,0:T(8,128)S(1)} collective-permute-done((f32[32,16,128]{2,1,0:T(8,128)S(1)}, f32[32,16,128]{2,1,0:T(8,128)S(1)}, u32[]{:S(2)}, u32[]{:S(2)}) %collective-permute-start.1) | collective-permute-done | bytes 262176 | tf_op jit(solution)/shard_map/while/body/eval_jaxpr/ppermute | solution.py:40
  612.1 7.4 %collective-permute-done.1 = f32[32,16,128]{2,1,0:T(8,128)S(1)} collective-permute-done((f32[32,16,128]{2,1,0:T(8,128)S(1)}, f32[32,16,128]{2,1,0:T(8,128)S(1)}, u32[]{:S(2)}, u32[]{:S(2)}) %collective-permute-start.1) | collective-permute-done | bytes 262176 | tf_op jit(solution)/shard_map/while/body/eval_jaxpr/ppermute | solution.py:40
  625.4 8.0 %collective-permute-done.2 = f32[32,16,128]{2,1,0:T(8,128)} collective-permute-done((f32[32,16,128]{2,1,0:T(8,128)S(1)}, f32[32,16,128]{2,1,0:T(8,128)}, u32[]{:S(2)}, u32[]{:S(2)}) %collective-permute-start.2) | collective-permute-done | bytes 262176 | tf_op jit(solution)/shard_map/ppermute | solution.py:40
  633.3 6.3 all-to-all-start
  641.4 17.8 %all-to-all-done = f32[32,1,16,128]{3,2,1,0:T(8,128)S(1)} async-done(((f32[32,1,16,128]{3,2,1,0:T(8,128)}), f32[32,1,16,128]{3,2,1,0:T(8,128)S(1)}, u32[]{:S(2)}, u32[]{:S(2)}) %all-to-all-start) | async-done | bytes 262176 | tf_op jit(solution)/shard_map/all_to_all | solution.py:50
  (605 shorter events, 220.3 us)
Async XLA Ops:
  7.2 191.7 %all-gather.5.cloned.1.call-start = ((), (), s32[]{:S(2)}) async-start(), calls=%async_computation.1 | async-start | bytes 2228224 | tf_op jit(solution)/shard_map/all_gather | solution.py:124
  379.3 10.6 %collective-permute-start = (bf16[32,16,128]{2,1,0:T(8,128)(2,1)S(1)}, bf16[32,16,128]{2,1,0:T(8,128)(2,1)S(1)}, u32[]{:S(2)}, u32[]{:S(2)}) collective-permute-start(bf16[32,16,128]{2,1,0:T(8,128)(2,1)S(1)} %copy.38), channel_id=1, source_target_pairs={{0,32},{32,64},{64,96},{96,128},{128,160},{160,192},{192,224},{224... | collective-permute-start | bytes 393224 | tf_op jit(solution)/shard_map/while/body/eval_jaxpr/ppermute | solution.py:40
  385.4 9.8 %collective-permute-start.1 = (f32[32,16,128]{2,1,0:T(8,128)S(1)}, f32[32,16,128]{2,1,0:T(8,128)S(1)}, u32[]{:S(2)}, u32[]{:S(2)}) collective-permute-start(f32[32,16,128]{2,1,0:T(8,128)S(1)} %add.300), channel_id=1, source_target_pairs={{0,32},{32,64},{64,96},{96,128},{128,160},{160,192},{192,224},{224... | collective-permute-start | bytes 786440 | tf_op jit(solution)/shard_map/while/body/eval_jaxpr/ppermute | solution.py:40
  395.2 8.6 %collective-permute-start = (bf16[32,16,128]{2,1,0:T(8,128)(2,1)S(1)}, bf16[32,16,128]{2,1,0:T(8,128)(2,1)S(1)}, u32[]{:S(2)}, u32[]{:S(2)}) collective-permute-start(bf16[32,16,128]{2,1,0:T(8,128)(2,1)S(1)} %copy.38), channel_id=1, source_target_pairs={{0,32},{32,64},{64,96},{96,128},{128,160},{160,192},{192,224},{224... | collective-permute-start | bytes 393224 | tf_op jit(solution)/shard_map/while/body/eval_jaxpr/ppermute | solution.py:40
  401.4 9.8 %collective-permute-start.1 = (f32[32,16,128]{2,1,0:T(8,128)S(1)}, f32[32,16,128]{2,1,0:T(8,128)S(1)}, u32[]{:S(2)}, u32[]{:S(2)}) collective-permute-start(f32[32,16,128]{2,1,0:T(8,128)S(1)} %add.300), channel_id=1, source_target_pairs={{0,32},{32,64},{64,96},{96,128},{128,160},{160,192},{192,224},{224... | collective-permute-start | bytes 786440 | tf_op jit(solution)/shard_map/while/body/eval_jaxpr/ppermute | solution.py:40
  411.2 8.6 %collective-permute-start = (bf16[32,16,128]{2,1,0:T(8,128)(2,1)S(1)}, bf16[32,16,128]{2,1,0:T(8,128)(2,1)S(1)}, u32[]{:S(2)}, u32[]{:S(2)}) collective-permute-start(bf16[32,16,128]{2,1,0:T(8,128)(2,1)S(1)} %copy.38), channel_id=1, source_target_pairs={{0,32},{32,64},{64,96},{96,128},{128,160},{160,192},{192,224},{224... | collective-permute-start | bytes 393224 | tf_op jit(solution)/shard_map/while/body/eval_jaxpr/ppermute | solution.py:40
  417.4 9.8 %collective-permute-start.1 = (f32[32,16,128]{2,1,0:T(8,128)S(1)}, f32[32,16,128]{2,1,0:T(8,128)S(1)}, u32[]{:S(2)}, u32[]{:S(2)}) collective-permute-start(f32[32,16,128]{2,1,0:T(8,128)S(1)} %add.300), channel_id=1, source_target_pairs={{0,32},{32,64},{64,96},{96,128},{128,160},{160,192},{192,224},{224... | collective-permute-start | bytes 786440 | tf_op jit(solution)/shard_map/while/body/eval_jaxpr/ppermute | solution.py:40
  427.2 8.6 %collective-permute-start = (bf16[32,16,128]{2,1,0:T(8,128)(2,1)S(1)}, bf16[32,16,128]{2,1,0:T(8,128)(2,1)S(1)}, u32[]{:S(2)}, u32[]{:S(2)}) collective-permute-start(bf16[32,16,128]{2,1,0:T(8,128)(2,1)S(1)} %copy.38), channel_id=1, source_target_pairs={{0,32},{32,64},{64,96},{96,128},{128,160},{160,192},{192,224},{224... | collective-permute-start | bytes 393224 | tf_op jit(solution)/shard_map/while/body/eval_jaxpr/ppermute | solution.py:40
  433.5 9.8 %collective-permute-start.1 = (f32[32,16,128]{2,1,0:T(8,128)S(1)}, f32[32,16,128]{2,1,0:T(8,128)S(1)}, u32[]{:S(2)}, u32[]{:S(2)}) collective-permute-start(f32[32,16,128]{2,1,0:T(8,128)S(1)} %add.300), channel_id=1, source_target_pairs={{0,32},{32,64},{64,96},{96,128},{128,160},{160,192},{192,224},{224... | collective-permute-start | bytes 786440 | tf_op jit(solution)/shard_map/while/body/eval_jaxpr/ppermute | solution.py:40
  443.3 8.6 %collective-permute-start = (bf16[32,16,128]{2,1,0:T(8,128)(2,1)S(1)}, bf16[32,16,128]{2,1,0:T(8,128)(2,1)S(1)}, u32[]{:S(2)}, u32[]{:S(2)}) collective-permute-start(bf16[32,16,128]{2,1,0:T(8,128)(2,1)S(1)} %copy.38), channel_id=1, source_target_pairs={{0,32},{32,64},{64,96},{96,128},{128,160},{160,192},{192,224},{224... | collective-permute-start | bytes 393224 | tf_op jit(solution)/shard_map/while/body/eval_jaxpr/ppermute | solution.py:40
  449.5 9.8 %collective-permute-start.1 = (f32[32,16,128]{2,1,0:T(8,128)S(1)}, f32[32,16,128]{2,1,0:T(8,128)S(1)}, u32[]{:S(2)}, u32[]{:S(2)}) collective-permute-start(f32[32,16,128]{2,1,0:T(8,128)S(1)} %add.300), channel_id=1, source_target_pairs={{0,32},{32,64},{64,96},{96,128},{128,160},{160,192},{192,224},{224... | collective-permute-start | bytes 786440 | tf_op jit(solution)/shard_map/while/body/eval_jaxpr/ppermute | solution.py:40
  459.3 8.6 %collective-permute-start = (bf16[32,16,128]{2,1,0:T(8,128)(2,1)S(1)}, bf16[32,16,128]{2,1,0:T(8,128)(2,1)S(1)}, u32[]{:S(2)}, u32[]{:S(2)}) collective-permute-start(bf16[32,16,128]{2,1,0:T(8,128)(2,1)S(1)} %copy.38), channel_id=1, source_target_pairs={{0,32},{32,64},{64,96},{96,128},{128,160},{160,192},{192,224},{224... | collective-permute-start | bytes 393224 | tf_op jit(solution)/shard_map/while/body/eval_jaxpr/ppermute | solution.py:40
  465.5 9.8 %collective-permute-start.1 = (f32[32,16,128]{2,1,0:T(8,128)S(1)}, f32[32,16,128]{2,1,0:T(8,128)S(1)}, u32[]{:S(2)}, u32[]{:S(2)}) collective-permute-start(f32[32,16,128]{2,1,0:T(8,128)S(1)} %add.300), channel_id=1, source_target_pairs={{0,32},{32,64},{64,96},{96,128},{128,160},{160,192},{192,224},{224... | collective-permute-start | bytes 786440 | tf_op jit(solution)/shard_map/while/body/eval_jaxpr/ppermute | solution.py:40
  475.3 8.6 %collective-permute-start = (bf16[32,16,128]{2,1,0:T(8,128)(2,1)S(1)}, bf16[32,16,128]{2,1,0:T(8,128)(2,1)S(1)}, u32[]{:S(2)}, u32[]{:S(2)}) collective-permute-start(bf16[32,16,128]{2,1,0:T(8,128)(2,1)S(1)} %copy.38), channel_id=1, source_target_pairs={{0,32},{32,64},{64,96},{96,128},{128,160},{160,192},{192,224},{224... | collective-permute-start | bytes 393224 | tf_op jit(solution)/shard_map/while/body/eval_jaxpr/ppermute | solution.py:40
  481.5 9.8 %collective-permute-start.1 = (f32[32,16,128]{2,1,0:T(8,128)S(1)}, f32[32,16,128]{2,1,0:T(8,128)S(1)}, u32[]{:S(2)}, u32[]{:S(2)}) collective-permute-start(f32[32,16,128]{2,1,0:T(8,128)S(1)} %add.300), channel_id=1, source_target_pairs={{0,32},{32,64},{64,96},{96,128},{128,160},{160,192},{192,224},{224... | collective-permute-start | bytes 786440 | tf_op jit(solution)/shard_map/while/body/eval_jaxpr/ppermute | solution.py:40
  491.3 8.6 %collective-permute-start = (bf16[32,16,128]{2,1,0:T(8,128)(2,1)S(1)}, bf16[32,16,128]{2,1,0:T(8,128)(2,1)S(1)}, u32[]{:S(2)}, u32[]{:S(2)}) collective-permute-start(bf16[32,16,128]{2,1,0:T(8,128)(2,1)S(1)} %copy.38), channel_id=1, source_target_pairs={{0,32},{32,64},{64,96},{96,128},{128,160},{160,192},{192,224},{224... | collective-permute-start | bytes 393224 | tf_op jit(solution)/shard_map/while/body/eval_jaxpr/ppermute | solution.py:40
  497.6 9.8 %collective-permute-start.1 = (f32[32,16,128]{2,1,0:T(8,128)S(1)}, f32[32,16,128]{2,1,0:T(8,128)S(1)}, u32[]{:S(2)}, u32[]{:S(2)}) collective-permute-start(f32[32,16,128]{2,1,0:T(8,128)S(1)} %add.300), channel_id=1, source_target_pairs={{0,32},{32,64},{64,96},{96,128},{128,160},{160,192},{192,224},{224... | collective-permute-start | bytes 786440 | tf_op jit(solution)/shard_map/while/body/eval_jaxpr/ppermute | solution.py:40
  507.4 8.6 %collective-permute-start = (bf16[32,16,128]{2,1,0:T(8,128)(2,1)S(1)}, bf16[32,16,128]{2,1,0:T(8,128)(2,1)S(1)}, u32[]{:S(2)}, u32[]{:S(2)}) collective-permute-start(bf16[32,16,128]{2,1,0:T(8,128)(2,1)S(1)} %copy.38), channel_id=1, source_target_pairs={{0,32},{32,64},{64,96},{96,128},{128,160},{160,192},{192,224},{224... | collective-permute-start | bytes 393224 | tf_op jit(solution)/shard_map/while/body/eval_jaxpr/ppermute | solution.py:40
  513.6 9.8 %collective-permute-start.1 = (f32[32,16,128]{2,1,0:T(8,128)S(1)}, f32[32,16,128]{2,1,0:T(8,128)S(1)}, u32[]{:S(2)}, u32[]{:S(2)}) collective-permute-start(f32[32,16,128]{2,1,0:T(8,128)S(1)} %add.300), channel_id=1, source_target_pairs={{0,32},{32,64},{64,96},{96,128},{128,160},{160,192},{192,224},{224... | collective-permute-start | bytes 786440 | tf_op jit(solution)/shard_map/while/body/eval_jaxpr/ppermute | solution.py:40
  523.4 8.6 %collective-permute-start = (bf16[32,16,128]{2,1,0:T(8,128)(2,1)S(1)}, bf16[32,16,128]{2,1,0:T(8,128)(2,1)S(1)}, u32[]{:S(2)}, u32[]{:S(2)}) collective-permute-start(bf16[32,16,128]{2,1,0:T(8,128)(2,1)S(1)} %copy.38), channel_id=1, source_target_pairs={{0,32},{32,64},{64,96},{96,128},{128,160},{160,192},{192,224},{224... | collective-permute-start | bytes 393224 | tf_op jit(solution)/shard_map/while/body/eval_jaxpr/ppermute | solution.py:40
  529.6 9.8 %collective-permute-start.1 = (f32[32,16,128]{2,1,0:T(8,128)S(1)}, f32[32,16,128]{2,1,0:T(8,128)S(1)}, u32[]{:S(2)}, u32[]{:S(2)}) collective-permute-start(f32[32,16,128]{2,1,0:T(8,128)S(1)} %add.300), channel_id=1, source_target_pairs={{0,32},{32,64},{64,96},{96,128},{128,160},{160,192},{192,224},{224... | collective-permute-start | bytes 786440 | tf_op jit(solution)/shard_map/while/body/eval_jaxpr/ppermute | solution.py:40
  539.4 8.6 %collective-permute-start = (bf16[32,16,128]{2,1,0:T(8,128)(2,1)S(1)}, bf16[32,16,128]{2,1,0:T(8,128)(2,1)S(1)}, u32[]{:S(2)}, u32[]{:S(2)}) collective-permute-start(bf16[32,16,128]{2,1,0:T(8,128)(2,1)S(1)} %copy.38), channel_id=1, source_target_pairs={{0,32},{32,64},{64,96},{96,128},{128,160},{160,192},{192,224},{224... | collective-permute-start | bytes 393224 | tf_op jit(solution)/shard_map/while/body/eval_jaxpr/ppermute | solution.py:40
  545.6 9.8 %collective-permute-start.1 = (f32[32,16,128]{2,1,0:T(8,128)S(1)}, f32[32,16,128]{2,1,0:T(8,128)S(1)}, u32[]{:S(2)}, u32[]{:S(2)}) collective-permute-start(f32[32,16,128]{2,1,0:T(8,128)S(1)} %add.300), channel_id=1, source_target_pairs={{0,32},{32,64},{64,96},{96,128},{128,160},{160,192},{192,224},{224... | collective-permute-start | bytes 786440 | tf_op jit(solution)/shard_map/while/body/eval_jaxpr/ppermute | solution.py:40
  561.7 9.8 %collective-permute-start.1 = (f32[32,16,128]{2,1,0:T(8,128)S(1)}, f32[32,16,128]{2,1,0:T(8,128)S(1)}, u32[]{:S(2)}, u32[]{:S(2)}) collective-permute-start(f32[32,16,128]{2,1,0:T(8,128)S(1)} %add.300), channel_id=1, source_target_pairs={{0,32},{32,64},{64,96},{96,128},{128,160},{160,192},{192,224},{224... | collective-permute-start | bytes 786440 | tf_op jit(solution)/shard_map/while/body/eval_jaxpr/ppermute | solution.py:40
  571.5 8.6 %collective-permute-start = (bf16[32,16,128]{2,1,0:T(8,128)(2,1)S(1)}, bf16[32,16,128]{2,1,0:T(8,128)(2,1)S(1)}, u32[]{:S(2)}, u32[]{:S(2)}) collective-permute-start(bf16[32,16,128]{2,1,0:T(8,128)(2,1)S(1)} %copy.38), channel_id=1, source_target_pairs={{0,32},{32,64},{64,96},{96,128},{128,160},{160,192},{192,224},{224... | collective-permute-start | bytes 393224 | tf_op jit(solution)/shard_map/while/body/eval_jaxpr/ppermute | solution.py:40
  577.7 9.8 %collective-permute-start.1 = (f32[32,16,128]{2,1,0:T(8,128)S(1)}, f32[32,16,128]{2,1,0:T(8,128)S(1)}, u32[]{:S(2)}, u32[]{:S(2)}) collective-permute-start(f32[32,16,128]{2,1,0:T(8,128)S(1)} %add.300), channel_id=1, source_target_pairs={{0,32},{32,64},{64,96},{96,128},{128,160},{160,192},{192,224},{224... | collective-permute-start | bytes 786440 | tf_op jit(solution)/shard_map/while/body/eval_jaxpr/ppermute | solution.py:40
  587.5 8.6 %collective-permute-start = (bf16[32,16,128]{2,1,0:T(8,128)(2,1)S(1)}, bf16[32,16,128]{2,1,0:T(8,128)(2,1)S(1)}, u32[]{:S(2)}, u32[]{:S(2)}) collective-permute-start(bf16[32,16,128]{2,1,0:T(8,128)(2,1)S(1)} %copy.38), channel_id=1, source_target_pairs={{0,32},{32,64},{64,96},{96,128},{128,160},{160,192},{192,224},{224... | collective-permute-start | bytes 393224 | tf_op jit(solution)/shard_map/while/body/eval_jaxpr/ppermute | solution.py:40
  593.7 9.8 %collective-permute-start.1 = (f32[32,16,128]{2,1,0:T(8,128)S(1)}, f32[32,16,128]{2,1,0:T(8,128)S(1)}, u32[]{:S(2)}, u32[]{:S(2)}) collective-permute-start(f32[32,16,128]{2,1,0:T(8,128)S(1)} %add.300), channel_id=1, source_target_pairs={{0,32},{32,64},{64,96},{96,128},{128,160},{160,192},{192,224},{224... | collective-permute-start | bytes 786440 | tf_op jit(solution)/shard_map/while/body/eval_jaxpr/ppermute | solution.py:40
  603.5 8.6 %collective-permute-start = (bf16[32,16,128]{2,1,0:T(8,128)(2,1)S(1)}, bf16[32,16,128]{2,1,0:T(8,128)(2,1)S(1)}, u32[]{:S(2)}, u32[]{:S(2)}) collective-permute-start(bf16[32,16,128]{2,1,0:T(8,128)(2,1)S(1)} %copy.38), channel_id=1, source_target_pairs={{0,32},{32,64},{64,96},{96,128},{128,160},{160,192},{192,224},{224... | collective-permute-start | bytes 393224 | tf_op jit(solution)/shard_map/while/body/eval_jaxpr/ppermute | solution.py:40
  609.7 9.8 %collective-permute-start.1 = (f32[32,16,128]{2,1,0:T(8,128)S(1)}, f32[32,16,128]{2,1,0:T(8,128)S(1)}, u32[]{:S(2)}, u32[]{:S(2)}) collective-permute-start(f32[32,16,128]{2,1,0:T(8,128)S(1)} %add.300), channel_id=1, source_target_pairs={{0,32},{32,64},{64,96},{96,128},{128,160},{160,192},{192,224},{224... | collective-permute-start | bytes 786440 | tf_op jit(solution)/shard_map/while/body/eval_jaxpr/ppermute | solution.py:40
  623.4 9.9 %collective-permute-start.2 = (f32[32,16,128]{2,1,0:T(8,128)S(1)}, f32[32,16,128]{2,1,0:T(8,128)}, u32[]{:S(2)}, u32[]{:S(2)}) collective-permute-start(f32[32,16,128]{2,1,0:T(8,128)S(1)} %add.247), channel_id=1, source_target_pairs={{0,32},{32,64},{64,96},{96,128},{128,160},{160,192},{192,224},{224... | collective-permute-start | bytes 786440 | tf_op jit(solution)/shard_map/ppermute | solution.py:40
  633.3 25.9 %all-to-all-start = ((f32[32,1,16,128]{3,2,1,0:T(8,128)}), f32[32,1,16,128]{3,2,1,0:T(8,128)S(1)}, u32[]{:S(2)}, u32[]{:S(2)}) async-start(f32[32,1,16,128]{3,2,1,0:T(8,128)} %bitcast.32), calls=%async_computation | async-start | bytes 524288 | tf_op jit(solution)/shard_map/all_to_all | solution.py:50
  (18 other events, 297.3 us)
Sparse Core Ops, SparseCore 0:
  94.6 31.2 all-gather.4
where the time goes:
time: 676 us; the launch traced here: 668 us
  blocking collectives  292 us (43%)
  waiting for transfers between devices  135 us (20%)
  matrix products  88 us (13%)
  starting transfers between devices  69.9 us (10%)
  other arithmetic  33.9 us (5%)
  local copies, waits for them, and re-layouts  29.3 us (4%)
  between operations  18 us (3%)
    ppermute x31, waiting for transfers between devices, from_behind(): return lax.ppermute(value, axis, pairs)  117 us
    all_gather x1, blocking collectives, on_device(): lax.all_gather(queries, GROUP, axis=0, tiled=True)  87.3 us
    all_gather x1, blocking collectives, side_by_side(): lax.all_gather(both, axis, axis=dim, tiled=True)  70.5 us
    ppermute x31, starting transfers between devices, from_behind(): return lax.ppermute(value, axis, pairs)  63.5 us
    dot_general x64, matrix products, masked_logits(): lax.dot_general(row_block, lone_document, (((1,), (1,)), ((), ())), prefe...  62.4 us
    pmax x5, blocking collectives, over_axes(): return functools.reduce(lax.pmax, axes, x)  54.4 us
    psum x5, blocking collectives, one_axis_at_a_time(): x = lax.psum(x, axis)  51.7 us
    broadcast_in_dim x32, other arithmetic, masked_logits(): jnp.where(live_image_embeddings[None, :] > 0, similarity_matrix / relaxat...  24.4 us
  transfers between devices with their start and end apart: 33, of which 17 were waited for; matrix products, arithmetic and copies ran while one was open for 11% of the time, Pallas kernels for 0%

commit v1 on v0

--- a/solution.py
+++ b/solution.py
@@ -11,6 +11,13 @@
 BLK_GROUP = ("blk_0", "blk_1", "blk_2", "group_0", "group_1")
 relaxation_scale_factor = 0.5
 guarded_floor_entry = -1e30
+
+
+def swapped_in(x, mesh_axis, dim):
+    peers = lax.axis_size(mesh_axis)
+    tiles = jnp.stack([x for _ in range(peers)])
+    tiles = lax.all_to_all(tiles, mesh_axis, split_axis=0, concat_axis=0)
+    return jnp.concatenate(tiles, axis=dim)
 
 
 def side_by_side(arrays, axis, dim, along):
@@ -72,7 +79,7 @@
     total_queries = bundle_size * blocks
     natural_logarithm_lengths = jnp.log(jnp.sum(page_mask.astype(jnp.float32), axis=1))
     bundle_vectors, bundle_masks, bundle_targets = (
-        lax.all_gather(queries, GROUP, axis=0, tiled=True),
+        swapped_in(queries, GROUP, 0),
         *side_by_side((query_mask, positive), GROUP, 0, 1),
     )
 

time: 676 us -> 533 us (0.79)
  matrix products: 88 us -> 26.7 us
  blocking collectives: 292 us -> 241 us
  other arithmetic: 33.9 us -> 10.5 us
    all_gather x1 -> x0, blocking collectives: 87.3 us -> none  [on_device(): lax.all_gather(queries, GROUP, axis=0, tiled=True)]
    dot_general x64, matrix products: 62.4 us -> 14 us  [masked_logits(): lax.dot_general(row_block, lone_document, (((1,), (1,)), ((), ())), prefe...]
    all_to_all x0 -> x1, blocking collectives: none -> 35.3 us  [swapped_in(): tiles = lax.all_to_all(tiles, mesh_axis, split_axis=0, concat_axis=0)]
    broadcast_in_dim x32, other arithmetic: 24.4 us -> 1 us  [masked_logits(): jnp.where(live_image_embeddings[None, :] > 0, similarity_matrix / relaxat...]
    dot_general x32, matrix products: 18.2 us -> 5.32 us  [gradient_terms(): jnp.dot(factor, page_vectors[number], preferred_element_type=jnp.float32)]
  transfers between devices with their start and end apart: 33 -> 33, of which waited for: 17 -> 32; matrix products, arithmetic and copies ran while one was open for 11% -> 5% of each run, Pallas kernels for 0% -> 0%
where the time goes in v1:
time: 533 us; the launch traced here: 531 us
  blocking collectives  241 us (45%)
  waiting for transfers between devices  135 us (25%)
  starting transfers between devices  68 us (13%)
  local copies, waits for them, and re-layouts  30 us (6%)
  matrix products  26.7 us (5%)
  between operations  18 us (3%)
  other arithmetic  10.5 us (2%)
    ppermute x31, waiting for transfers between devices, from_behind(): return lax.ppermute(value, axis, pairs)  117 us
    all_gather x1, blocking collectives, side_by_side(): lax.all_gather(both, axis, axis=dim, tiled=True)  71.2 us
    ppermute x31, starting transfers between devices, from_behind(): return lax.ppermute(value, axis, pairs)  61.6 us
    pmax x5, blocking collectives, over_axes(): return functools.reduce(lax.pmax, axes, x)  53.6 us
    psum x5, blocking collectives, one_axis_at_a_time(): x = lax.psum(x, axis)  52.5 us
    all_to_all x1, blocking collectives, swapped_in(): tiles = lax.all_to_all(tiles, mesh_axis, split_axis=0, concat_axis=0)  35.3 us
    all_gather x1, blocking collectives, on_device(): lax.all_gather(bundle_masks, BLK, axis=0, tiled=True)  20.1 us
    all_to_all x1, waiting for transfers between devices, sum_at_owner(): pieces = lax.all_to_all(cut_along(x, dim, size), axis, 0, 0, tiled=True)  17.8 us
  transfers between devices with their start and end apart: 33, of which 32 were waited for; matrix products, arithmetic and copies ran while one was open for 5% of the time, Pallas kernels for 0%

profile of v1, /device:TPU:2, one launch (start us, length us, event | category | flops | bytes accessed | tf_op | source)
XLA Modules:
  0.0 530.9 jit_solution(1759099171696694886)
XLA Ops:
  7.9 35.3 %all_to_all.10 = bf16[32,1,16,128]{3,2,1,0:T(8,128)(2,1)} all-to-all(bf16[32,1,16,128]{3,2,1,0:T(8,128)(2,1)S(1)} %stack.10), channel_id=1, replica_groups=mesh['blk_0'=2,'blk_1'=4,'blk_2'=2,'group_0'=2,'group_1'=16] {'group_0',..., dimensions={0} | all-to-all | bytes 262144 | tf_op jit(solution)/shard_map/all_to_all | solution.py:19
  44.7 71.2 %all-gather.2 = s32[32,1,17]{2,1,0:T(1,128)S(1)} all-gather(s32[1,1,17]{2,1,0:T(1,128)S(1)} %add_bitcast_fusion), channel_id=1, replica_groups=mesh['blk_0'=2,'blk_1'=4,'blk_2'=2,'group_0'=2,'group_1'=16] {'group_0',..., dimensions={0}, use_global_device_ids=true | all-gather | bytes 2244 | tf_op jit(solution)/shard_map/all_gather | solution.py:26
  116.0 20.1 %all-gather.3 = s32[16,32,16]{1,2,0:T(8,128)S(1)} all-gather(s32[1,32,16]{1,2,0:T(8,128)S(1)} %copy.11), channel_id=1, replica_groups=mesh['blk_0'=2,'blk_1'=4,'blk_2'=2,'group_0'=2,'group_1'=16] {'blk_0','b..., dimensions={0}, use_global_device_ids=true | all-gather | bytes 34816 | tf_op jit(solution)/shard_map/all_gather | solution.py:132
  139.6 8.0 %all-reduce = s32[512]{0:T(512)S(1)} all-reduce(s32[512]{0:T(512)S(1)} %dynamic-update-slice.26), channel_id=3, replica_groups=mesh['blk_0'=2,'blk_1'=4,'blk_2'=2,'group_0'=2,'group_1'=16] {'blk_0','b..., use_global_device_ids=true, to_apply=%add | all-reduce | flops 512 | bytes 4096
  148.5 36.2 %while.38 = (s32[]{:T(128)}, f32[512,2]{0,1:T(2,128)S(1)}, f32[512,16,2]{1,0,2:T(8,128)S(1)}, s32[2,128]{1,0:T(2,128)S(1)}, bf16[512,16,128]{2,1,0:T(8,128)(2,1)...) while((s32[]{:T(128)}, f32[512,2]{0,1:T(2,128)S(1)}, ...), condition=%wide.region_7.8_spmd, body=%wide.region_1.7_spmd.sunk | while | flops 34213060 | bytes 1821107 | solution.py:115
  184.7 4.9 pmax.35
  189.6 11.6 %pmax.36 = f32[512]{0:T(512)S(1)} all-reduce(f32[512]{0:T(512)S(1)} %pmax.35), channel_id=1, replica_groups=mesh['blk_0'=2,'blk_1'=4,'blk_2'=2,'group_0'=2,'group_1'=16] {'blk_1'}, use_global_device_ids=true, to_apply=%region_10.11 | all-reduce | flops 512 | bytes 4096 | tf_op jit(solution)/shard_map/pmax | solution.py:35
  203.7 6.4 %pmax.38 = f32[512]{0:T(512)S(1)} all-reduce(f32[512]{0:T(512)S(1)} %pmax.37), channel_id=1, replica_groups=mesh['blk_0'=2,'blk_1'=4,'blk_2'=2,'group_0'=2,'group_1'=16] {'group_0'}, use_global_device_ids=true, to_apply=%region_12.13 | all-reduce | flops 512 | bytes 4096 | tf_op jit(solution)/shard_map/pmax | solution.py:35
  210.1 28.2 %pmax.39 = f32[512]{0:T(512)S(1)} all-reduce(f32[512]{0:T(512)S(1)} %pmax.38), channel_id=1, replica_groups=mesh['blk_0'=2,'blk_1'=4,'blk_2'=2,'group_0'=2,'group_1'=16] {'group_1'}, use_global_device_ids=true, to_apply=%region_13.14 | all-reduce | flops 512 | bytes 4096 | tf_op jit(solution)/shard_map/pmax | solution.py:35
  239.0 5.5 %all-reduce.5 = (f32[512]{0:T(512)S(1)}, f32[]{:T(128)}) all-reduce(f32[512]{0:T(512)S(1)} %get-tuple-element.459, f32[]{:T(128)} %get-tuple-element.458), channel_id=1, replica_groups=mesh['blk_0'=2,'blk_1'=4,'blk_2'=2,'group_0'=2,'group_1'=16] {'blk_0'}, use_global_device_ids=true, to_apply=%region_15.16 | all-reduce | flops 513 | bytes 4104 | tf_op jit(solution)/shard_map/psum | solution.py:40
  244.5 8.3 %all-reduce.2 = (f32[512]{0:T(512)S(1)}, f32[]{:T(128)}) all-reduce(f32[512]{0:T(512)S(1)} %get-tuple-element.502, f32[]{:T(128)} %get-tuple-element.503), channel_id=1, replica_groups=mesh['blk_0'=2,'blk_1'=4,'blk_2'=2,'group_0'=2,'group_1'=16] {'blk_1'}, use_global_device_ids=true, to_apply=%region_16.17 | all-reduce | flops 513 | bytes 4104 | tf_op jit(solution)/shard_map/psum | solution.py:40
  256.0 7.0 %all-reduce.3 = (f32[512]{0:T(512)S(1)}, f32[]{:T(128)}) all-reduce(f32[512]{0:T(512)S(1)} %get-tuple-element.500, f32[]{:T(128)} %get-tuple-element.501), channel_id=1, replica_groups=mesh['blk_0'=2,'blk_1'=4,'blk_2'=2,'group_0'=2,'group_1'=16] {'group_0'}, use_global_device_ids=true, to_apply=%region_18.19 | all-reduce | flops 513 | bytes 4104 | tf_op jit(solution)/shard_map/psum | solution.py:40
  263.0 28.4 %all-reduce.1 = (f32[512]{0:T(512)S(1)}, f32[]{:T(128)}) all-reduce(f32[512]{0:T(512)S(1)} %get-tuple-element.498, f32[]{:T(128)} %get-tuple-element.499), channel_id=1, replica_groups=mesh['blk_0'=2,'blk_1'=4,'blk_2'=2,'group_0'=2,'group_1'=16] {'group_1'}, use_global_device_ids=true, to_apply=%region_19.20 | all-reduce | flops 513 | bytes 4104 | tf_op jit(solution)/shard_map/psum | solution.py:40
  292.7 192.9 %while.39 = (s32[]{:T(128)}, bf16[32,16,128]{2,1,0:T(8,128)(2,1)S(1)}, f32[32,16,128]{2,1,0:T(8,128)S(1)}, f32[2,128,128]{2,1,0:T(8,128)S(1)}, s32[]{:T(128)}, /...) while((s32[]{:T(128)}, ...), condition=%wide.region_21.22_spmd, body=%wide.region_20.21_spmd.sunk | while | flops 101482768 | bytes 5171848 | solution.py:198
  301.1 4.5 collective-permute-done.1
  314.0 4.5 collective-permute-done.1
  326.8 4.5 collective-permute-done.1
  339.7 4.5 collective-permute-done.1
  352.6 4.4 collective-permute-done.1
  365.4 4.4 collective-permute-done.1
  378.3 4.4 collective-permute-done.1
  391.1 4.4 collective-permute-done.1
  404.0 4.4 collective-permute-done.1
  416.9 4.4 collective-permute-done.1
  429.7 4.4 collective-permute-done.1
  442.6 4.4 collective-permute-done.1
  455.4 4.4 collective-permute-done.1
  468.3 4.4 collective-permute-done.1
  481.2 4.4 collective-permute-done.1
  488.4 8.0 %collective-permute-done.2 = f32[32,16,128]{2,1,0:T(8,128)} collective-permute-done((f32[32,16,128]{2,1,0:T(8,128)S(1)}, f32[32,16,128]{2,1,0:T(8,128)}, u32[]{:S(2)}, u32[]{:S(2)}) %collective-permute-start.2) | collective-permute-done | bytes 262176 | tf_op jit(solution)/shard_map/ppermute | solution.py:47
  496.4 6.3 %all-to-all-start.1 = ((f32[32,1,16,128]{3,2,1,0:T(8,128)}), f32[32,1,16,128]{3,2,1,0:T(8,128)S(1)}, u32[]{:S(2)}, u32[]{:S(2)}) async-start(f32[32,1,16,128]{3,2,1,0:T(8,128)} %bitcast.35), calls=%async_computation.1 | async-start | bytes 524288 | tf_op jit(solution)/shard_map/all_to_all | solution.py:57
  504.5 17.8 %all-to-all-done.1 = f32[32,1,16,128]{3,2,1,0:T(8,128)S(1)} async-done(((f32[32,1,16,128]{3,2,1,0:T(8,128)}), f32[32,1,16,128]{3,2,1,0:T(8,128)S(1)}, u32[]{:S(2)}, u32[]{:S(2)}) %all-to-all-start.1) | async-done | bytes 262176 | tf_op jit(solution)/shard_map/all_to_all | solution.py:57
  (580 shorter events, 176.4 us)
Async XLA Ops:
  7.2 141.2 %all-gather.6.cloned.1.call-start = ((), (), s32[]{:S(2)}) async-start(), calls=%async_computation.2 | async-start | bytes 2228224 | tf_op jit(solution)/shard_map/all_gather | solution.py:131
  292.7 8.4 %collective-permute-start = (bf16[32,16,128]{2,1,0:T(8,128)(2,1)S(1)}, bf16[32,16,128]{2,1,0:T(8,128)(2,1)S(1)}, u32[]{:S(2)}, u32[]{:S(2)}) collective-permute-start(bf16[32,16,128]{2,1,0:T(8,128)(2,1)S(1)} %copy.38), channel_id=1, source_target_pairs={{0,32},{32,64},{64,96},{96,128},{128,160},{160,192},{192,224},{224... | collective-permute-start | bytes 393224 | tf_op jit(solution)/shard_map/while/body/eval_jaxpr/ppermute | solution.py:47
  295.8 9.8 %collective-permute-start.1 = (f32[32,16,128]{2,1,0:T(8,128)S(1)}, f32[32,16,128]{2,1,0:T(8,128)S(1)}, u32[]{:S(2)}, u32[]{:S(2)}) collective-permute-start(f32[32,16,128]{2,1,0:T(8,128)S(1)} %add.300), channel_id=1, source_target_pairs={{0,32},{32,64},{64,96},{96,128},{128,160},{160,192},{192,224},{224... | collective-permute-start | bytes 786440 | tf_op jit(solution)/shard_map/while/body/eval_jaxpr/ppermute | solution.py:47
  305.6 8.4 %collective-permute-start = (bf16[32,16,128]{2,1,0:T(8,128)(2,1)S(1)}, bf16[32,16,128]{2,1,0:T(8,128)(2,1)S(1)}, u32[]{:S(2)}, u32[]{:S(2)}) collective-permute-start(bf16[32,16,128]{2,1,0:T(8,128)(2,1)S(1)} %copy.38), channel_id=1, source_target_pairs={{0,32},{32,64},{64,96},{96,128},{128,160},{160,192},{192,224},{224... | collective-permute-start | bytes 393224 | tf_op jit(solution)/shard_map/while/body/eval_jaxpr/ppermute | solution.py:47
  308.6 9.8 %collective-permute-start.1 = (f32[32,16,128]{2,1,0:T(8,128)S(1)}, f32[32,16,128]{2,1,0:T(8,128)S(1)}, u32[]{:S(2)}, u32[]{:S(2)}) collective-permute-start(f32[32,16,128]{2,1,0:T(8,128)S(1)} %add.300), channel_id=1, source_target_pairs={{0,32},{32,64},{64,96},{96,128},{128,160},{160,192},{192,224},{224... | collective-permute-start | bytes 786440 | tf_op jit(solution)/shard_map/while/body/eval_jaxpr/ppermute | solution.py:47
  318.4 8.4 %collective-permute-start = (bf16[32,16,128]{2,1,0:T(8,128)(2,1)S(1)}, bf16[32,16,128]{2,1,0:T(8,128)(2,1)S(1)}, u32[]{:S(2)}, u32[]{:S(2)}) collective-permute-start(bf16[32,16,128]{2,1,0:T(8,128)(2,1)S(1)} %copy.38), channel_id=1, source_target_pairs={{0,32},{32,64},{64,96},{96,128},{128,160},{160,192},{192,224},{224... | collective-permute-start | bytes 393224 | tf_op jit(solution)/shard_map/while/body/eval_jaxpr/ppermute | solution.py:47
  321.5 9.8 %collective-permute-start.1 = (f32[32,16,128]{2,1,0:T(8,128)S(1)}, f32[32,16,128]{2,1,0:T(8,128)S(1)}, u32[]{:S(2)}, u32[]{:S(2)}) collective-permute-start(f32[32,16,128]{2,1,0:T(8,128)S(1)} %add.300), channel_id=1, source_target_pairs={{0,32},{32,64},{64,96},{96,128},{128,160},{160,192},{192,224},{224... | collective-permute-start | bytes 786440 | tf_op jit(solution)/shard_map/while/body/eval_jaxpr/ppermute | solution.py:47
  331.3 8.4 %collective-permute-start = (bf16[32,16,128]{2,1,0:T(8,128)(2,1)S(1)}, bf16[32,16,128]{2,1,0:T(8,128)(2,1)S(1)}, u32[]{:S(2)}, u32[]{:S(2)}) collective-permute-start(bf16[32,16,128]{2,1,0:T(8,128)(2,1)S(1)} %copy.38), channel_id=1, source_target_pairs={{0,32},{32,64},{64,96},{96,128},{128,160},{160,192},{192,224},{224... | collective-permute-start | bytes 393224 | tf_op jit(solution)/shard_map/while/body/eval_jaxpr/ppermute | solution.py:47
  334.3 9.8 %collective-permute-start.1 = (f32[32,16,128]{2,1,0:T(8,128)S(1)}, f32[32,16,128]{2,1,0:T(8,128)S(1)}, u32[]{:S(2)}, u32[]{:S(2)}) collective-permute-start(f32[32,16,128]{2,1,0:T(8,128)S(1)} %add.300), channel_id=1, source_target_pairs={{0,32},{32,64},{64,96},{96,128},{128,160},{160,192},{192,224},{224... | collective-permute-start | bytes 786440 | tf_op jit(solution)/shard_map/while/body/eval_jaxpr/ppermute | solution.py:47
  344.2 8.4 %collective-permute-start = (bf16[32,16,128]{2,1,0:T(8,128)(2,1)S(1)}, bf16[32,16,128]{2,1,0:T(8,128)(2,1)S(1)}, u32[]{:S(2)}, u32[]{:S(2)}) collective-permute-start(bf16[32,16,128]{2,1,0:T(8,128)(2,1)S(1)} %copy.38), channel_id=1, source_target_pairs={{0,32},{32,64},{64,96},{96,128},{128,160},{160,192},{192,224},{224... | collective-permute-start | bytes 393224 | tf_op jit(solution)/shard_map/while/body/eval_jaxpr/ppermute | solution.py:47
  347.2 9.8 %collective-permute-start.1 = (f32[32,16,128]{2,1,0:T(8,128)S(1)}, f32[32,16,128]{2,1,0:T(8,128)S(1)}, u32[]{:S(2)}, u32[]{:S(2)}) collective-permute-start(f32[32,16,128]{2,1,0:T(8,128)S(1)} %add.300), channel_id=1, source_target_pairs={{0,32},{32,64},{64,96},{96,128},{128,160},{160,192},{192,224},{224... | collective-permute-start | bytes 786440 | tf_op jit(solution)/shard_map/while/body/eval_jaxpr/ppermute | solution.py:47
  357.0 8.4 %collective-permute-start = (bf16[32,16,128]{2,1,0:T(8,128)(2,1)S(1)}, bf16[32,16,128]{2,1,0:T(8,128)(2,1)S(1)}, u32[]{:S(2)}, u32[]{:S(2)}) collective-permute-start(bf16[32,16,128]{2,1,0:T(8,128)(2,1)S(1)} %copy.38), channel_id=1, source_target_pairs={{0,32},{32,64},{64,96},{96,128},{128,160},{160,192},{192,224},{224... | collective-permute-start | bytes 393224 | tf_op jit(solution)/shard_map/while/body/eval_jaxpr/ppermute | solution.py:47
  360.1 9.8 %collective-permute-start.1 = (f32[32,16,128]{2,1,0:T(8,128)S(1)}, f32[32,16,128]{2,1,0:T(8,128)S(1)}, u32[]{:S(2)}, u32[]{:S(2)}) collective-permute-start(f32[32,16,128]{2,1,0:T(8,128)S(1)} %add.300), channel_id=1, source_target_pairs={{0,32},{32,64},{64,96},{96,128},{128,160},{160,192},{192,224},{224... | collective-permute-start | bytes 786440 | tf_op jit(solution)/shard_map/while/body/eval_jaxpr/ppermute | solution.py:47
  369.9 8.4 %collective-permute-start = (bf16[32,16,128]{2,1,0:T(8,128)(2,1)S(1)}, bf16[32,16,128]{2,1,0:T(8,128)(2,1)S(1)}, u32[]{:S(2)}, u32[]{:S(2)}) collective-permute-start(bf16[32,16,128]{2,1,0:T(8,128)(2,1)S(1)} %copy.38), channel_id=1, source_target_pairs={{0,32},{32,64},{64,96},{96,128},{128,160},{160,192},{192,224},{224... | collective-permute-start | bytes 393224 | tf_op jit(solution)/shard_map/while/body/eval_jaxpr/ppermute | solution.py:47
  372.9 9.8 %collective-permute-start.1 = (f32[32,16,128]{2,1,0:T(8,128)S(1)}, f32[32,16,128]{2,1,0:T(8,128)S(1)}, u32[]{:S(2)}, u32[]{:S(2)}) collective-permute-start(f32[32,16,128]{2,1,0:T(8,128)S(1)} %add.300), channel_id=1, source_target_pairs={{0,32},{32,64},{64,96},{96,128},{128,160},{160,192},{192,224},{224... | collective-permute-start | bytes 786440 | tf_op jit(solution)/shard_map/while/body/eval_jaxpr/ppermute | solution.py:47
  382.7 8.4 %collective-permute-start = (bf16[32,16,128]{2,1,0:T(8,128)(2,1)S(1)}, bf16[32,16,128]{2,1,0:T(8,128)(2,1)S(1)}, u32[]{:S(2)}, u32[]{:S(2)}) collective-permute-start(bf16[32,16,128]{2,1,0:T(8,128)(2,1)S(1)} %copy.38), channel_id=1, source_target_pairs={{0,32},{32,64},{64,96},{96,128},{128,160},{160,192},{192,224},{224... | collective-permute-start | bytes 393224 | tf_op jit(solution)/shard_map/while/body/eval_jaxpr/ppermute | solution.py:47
  385.8 9.8 %collective-permute-start.1 = (f32[32,16,128]{2,1,0:T(8,128)S(1)}, f32[32,16,128]{2,1,0:T(8,128)S(1)}, u32[]{:S(2)}, u32[]{:S(2)}) collective-permute-start(f32[32,16,128]{2,1,0:T(8,128)S(1)} %add.300), channel_id=1, source_target_pairs={{0,32},{32,64},{64,96},{96,128},{128,160},{160,192},{192,224},{224... | collective-permute-start | bytes 786440 | tf_op jit(solution)/shard_map/while/body/eval_jaxpr/ppermute | solution.py:47
  395.6 8.4 %collective-permute-start = (bf16[32,16,128]{2,1,0:T(8,128)(2,1)S(1)}, bf16[32,16,128]{2,1,0:T(8,128)(2,1)S(1)}, u32[]{:S(2)}, u32[]{:S(2)}) collective-permute-start(bf16[32,16,128]{2,1,0:T(8,128)(2,1)S(1)} %copy.38), channel_id=1, source_target_pairs={{0,32},{32,64},{64,96},{96,128},{128,160},{160,192},{192,224},{224... | collective-permute-start | bytes 393224 | tf_op jit(solution)/shard_map/while/body/eval_jaxpr/ppermute | solution.py:47
  398.6 9.8 %collective-permute-start.1 = (f32[32,16,128]{2,1,0:T(8,128)S(1)}, f32[32,16,128]{2,1,0:T(8,128)S(1)}, u32[]{:S(2)}, u32[]{:S(2)}) collective-permute-start(f32[32,16,128]{2,1,0:T(8,128)S(1)} %add.300), channel_id=1, source_target_pairs={{0,32},{32,64},{64,96},{96,128},{128,160},{160,192},{192,224},{224... | collective-permute-start | bytes 786440 | tf_op jit(solution)/shard_map/while/body/eval_jaxpr/ppermute | solution.py:47
  408.5 8.4 %collective-permute-start = (bf16[32,16,128]{2,1,0:T(8,128)(2,1)S(1)}, bf16[32,16,128]{2,1,0:T(8,128)(2,1)S(1)}, u32[]{:S(2)}, u32[]{:S(2)}) collective-permute-start(bf16[32,16,128]{2,1,0:T(8,128)(2,1)S(1)} %copy.38), channel_id=1, source_target_pairs={{0,32},{32,64},{64,96},{96,128},{128,160},{160,192},{192,224},{224... | collective-permute-start | bytes 393224 | tf_op jit(solution)/shard_map/while/body/eval_jaxpr/ppermute | solution.py:47
  411.5 9.8 %collective-permute-start.1 = (f32[32,16,128]{2,1,0:T(8,128)S(1)}, f32[32,16,128]{2,1,0:T(8,128)S(1)}, u32[]{:S(2)}, u32[]{:S(2)}) collective-permute-start(f32[32,16,128]{2,1,0:T(8,128)S(1)} %add.300), channel_id=1, source_target_pairs={{0,32},{32,64},{64,96},{96,128},{128,160},{160,192},{192,224},{224... | collective-permute-start | bytes 786440 | tf_op jit(solution)/shard_map/while/body/eval_jaxpr/ppermute | solution.py:47
  421.3 8.4 %collective-permute-start = (bf16[32,16,128]{2,1,0:T(8,128)(2,1)S(1)}, bf16[32,16,128]{2,1,0:T(8,128)(2,1)S(1)}, u32[]{:S(2)}, u32[]{:S(2)}) collective-permute-start(bf16[32,16,128]{2,1,0:T(8,128)(2,1)S(1)} %copy.38), channel_id=1, source_target_pairs={{0,32},{32,64},{64,96},{96,128},{128,160},{160,192},{192,224},{224... | collective-permute-start | bytes 393224 | tf_op jit(solution)/shard_map/while/body/eval_jaxpr/ppermute | solution.py:47
  424.4 9.8 %collective-permute-start.1 = (f32[32,16,128]{2,1,0:T(8,128)S(1)}, f32[32,16,128]{2,1,0:T(8,128)S(1)}, u32[]{:S(2)}, u32[]{:S(2)}) collective-permute-start(f32[32,16,128]{2,1,0:T(8,128)S(1)} %add.300), channel_id=1, source_target_pairs={{0,32},{32,64},{64,96},{96,128},{128,160},{160,192},{192,224},{224... | collective-permute-start | bytes 786440 | tf_op jit(solution)/shard_map/while/body/eval_jaxpr/ppermute | solution.py:47
  437.2 9.8 %collective-permute-start.1 = (f32[32,16,128]{2,1,0:T(8,128)S(1)}, f32[32,16,128]{2,1,0:T(8,128)S(1)}, u32[]{:S(2)}, u32[]{:S(2)}) collective-permute-start(f32[32,16,128]{2,1,0:T(8,128)S(1)} %add.300), channel_id=1, source_target_pairs={{0,32},{32,64},{64,96},{96,128},{128,160},{160,192},{192,224},{224... | collective-permute-start | bytes 786440 | tf_op jit(solution)/shard_map/while/body/eval_jaxpr/ppermute | solution.py:47
  447.0 8.4 %collective-permute-start = (bf16[32,16,128]{2,1,0:T(8,128)(2,1)S(1)}, bf16[32,16,128]{2,1,0:T(8,128)(2,1)S(1)}, u32[]{:S(2)}, u32[]{:S(2)}) collective-permute-start(bf16[32,16,128]{2,1,0:T(8,128)(2,1)S(1)} %copy.38), channel_id=1, source_target_pairs={{0,32},{32,64},{64,96},{96,128},{128,160},{160,192},{192,224},{224... | collective-permute-start | bytes 393224 | tf_op jit(solution)/shard_map/while/body/eval_jaxpr/ppermute | solution.py:47
  450.1 9.8 %collective-permute-start.1 = (f32[32,16,128]{2,1,0:T(8,128)S(1)}, f32[32,16,128]{2,1,0:T(8,128)S(1)}, u32[]{:S(2)}, u32[]{:S(2)}) collective-permute-start(f32[32,16,128]{2,1,0:T(8,128)S(1)} %add.300), channel_id=1, source_target_pairs={{0,32},{32,64},{64,96},{96,128},{128,160},{160,192},{192,224},{224... | collective-permute-start | bytes 786440 | tf_op jit(solution)/shard_map/while/body/eval_jaxpr/ppermute | solution.py:47
  459.9 8.4 %collective-permute-start = (bf16[32,16,128]{2,1,0:T(8,128)(2,1)S(1)}, bf16[32,16,128]{2,1,0:T(8,128)(2,1)S(1)}, u32[]{:S(2)}, u32[]{:S(2)}) collective-permute-start(bf16[32,16,128]{2,1,0:T(8,128)(2,1)S(1)} %copy.38), channel_id=1, source_target_pairs={{0,32},{32,64},{64,96},{96,128},{128,160},{160,192},{192,224},{224... | collective-permute-start | bytes 393224 | tf_op jit(solution)/shard_map/while/body/eval_jaxpr/ppermute | solution.py:47
  462.9 9.8 %collective-permute-start.1 = (f32[32,16,128]{2,1,0:T(8,128)S(1)}, f32[32,16,128]{2,1,0:T(8,128)S(1)}, u32[]{:S(2)}, u32[]{:S(2)}) collective-permute-start(f32[32,16,128]{2,1,0:T(8,128)S(1)} %add.300), channel_id=1, source_target_pairs={{0,32},{32,64},{64,96},{96,128},{128,160},{160,192},{192,224},{224... | collective-permute-start | bytes 786440 | tf_op jit(solution)/shard_map/while/body/eval_jaxpr/ppermute | solution.py:47
  472.8 8.4 %collective-permute-start = (bf16[32,16,128]{2,1,0:T(8,128)(2,1)S(1)}, bf16[32,16,128]{2,1,0:T(8,128)(2,1)S(1)}, u32[]{:S(2)}, u32[]{:S(2)}) collective-permute-start(bf16[32,16,128]{2,1,0:T(8,128)(2,1)S(1)} %copy.38), channel_id=1, source_target_pairs={{0,32},{32,64},{64,96},{96,128},{128,160},{160,192},{192,224},{224... | collective-permute-start | bytes 393224 | tf_op jit(solution)/shard_map/while/body/eval_jaxpr/ppermute | solution.py:47
  475.8 9.8 %collective-permute-start.1 = (f32[32,16,128]{2,1,0:T(8,128)S(1)}, f32[32,16,128]{2,1,0:T(8,128)S(1)}, u32[]{:S(2)}, u32[]{:S(2)}) collective-permute-start(f32[32,16,128]{2,1,0:T(8,128)S(1)} %add.300), channel_id=1, source_target_pairs={{0,32},{32,64},{64,96},{96,128},{128,160},{160,192},{192,224},{224... | collective-permute-start | bytes 786440 | tf_op jit(solution)/shard_map/while/body/eval_jaxpr/ppermute | solution.py:47
  486.5 9.9 %collective-permute-start.2 = (f32[32,16,128]{2,1,0:T(8,128)S(1)}, f32[32,16,128]{2,1,0:T(8,128)}, u32[]{:S(2)}, u32[]{:S(2)}) collective-permute-start(f32[32,16,128]{2,1,0:T(8,128)S(1)} %add.247), channel_id=1, source_target_pairs={{0,32},{32,64},{64,96},{96,128},{128,160},{160,192},{192,224},{224... | collective-permute-start | bytes 786440 | tf_op jit(solution)/shard_map/ppermute | solution.py:47
  496.4 25.9 %all-to-all-start.1 = ((f32[32,1,16,128]{3,2,1,0:T(8,128)}), f32[32,1,16,128]{3,2,1,0:T(8,128)S(1)}, u32[]{:S(2)}, u32[]{:S(2)}) async-start(f32[32,1,16,128]{3,2,1,0:T(8,128)} %bitcast.35), calls=%async_computation.1 | async-start | bytes 524288 | tf_op jit(solution)/shard_map/all_to_all | solution.py:57
  (5 other events, 453.6 us)
Sparse Core Ops, SparseCore 0:
  43.4 31.1 all-gather.5
